TPU v7x, 32 devices: a whole 2x2x4 slice. The times are simulated.
32 devices in a mesh: group: 8 (over z, x), peer: 4 (over y, core).
Axes of the slice: x: 2, y: 2, z: 4, core: 2. Of those that a mesh axis runs over, the one named last changes fastest.
Arguments:
- features: bfloat16 [12288, 1024], P(('group', 'peer')), may hold values from -6 to 6
- task_mask: int32 [12288], P(('group', 'peer')), may hold values from 0 to 65535, as said below
- tower_in: bfloat16 [16, 2048, 1024], P('peer', 'group'), may hold values from -0.1875 to 0.1875
- tower_bias: bfloat16 [16, 2048], P('peer', 'group'), may hold values from -5 to 5
- tower_head: bfloat16 [16, 2048], P('peer', 'group'), may hold values from -0.125 to 0.125
- head_bias: float32 [16], P('peer'), may hold values from -4 to 4
Outputs:
- predictions: float32 [12288, 16], P(('group', 'peer'))
Inputs may be any that keep to these rules, and one draw needn't show every extreme that they name: `task_mask`: only bits 0 to 15 are used. Among the 384 samples of one device (aligned blocks of 384), at most 176 have any one bit set; in every run of 4 blocks that one group holds, some task's bit is set exactly 176 times in each block.
All inputs are finite; a program needn't handle non-finite values.
Results may differ from a plain program's by a relative error of at most 0.0003.
Values may be sent and summed in bfloat16 or wider, within the bound.
A program may use at most 128 MiB of HBM per device.

v0:
```python
import functools

import jax
import jax.numpy as jnp
from jax import lax
from jax.experimental import pallas as pl
from jax.experimental.pallas import tpu as pltpu
from jax.sharding import PartitionSpec as P

MESH = pl.DeviceIdType.MESH
LANES = 128
PIECE_ROWS = 64
FIRST = 0
STEP_COLS = 256


def split_of_group(group, peers, weight_bytes, sample_bytes):
    sizes = [f for f in range(1, group + 1) if group % f == 0]

    def cost(f):
        return (f - 1) * weight_bytes + (group // f * peers - 1) * sample_bytes / 2

    return min(sizes, key=cost)


def kernel(
    outer, inner, peers,
    feat_ref, weight_ref, bias_ref, head_ref, hbias_ref, out_ref,
    x_buf, w_buf, b_buf, c_buf, part, ret,
    load_sem, x_recv, z_send, f_send, y_send, core_send, w_send, w_recv, b_send, b_recv,
    p_send, p_recv,
):
    rows, depth = feat_ref.shape
    towers, hidden, _ = weight_ref.shape
    piece = PIECE_ROWS
    pieces = rows // piece
    ys = peers // 2
    group_at, me = lax.axis_index("group"), lax.axis_index("peer")
    a, i = group_at // inner, group_at % inner
    y, c = me // 2, me % 2
    partner = y * 2 + (1 - c)

    def dev(a_to, i_to, p_to):
        return (a_to * inner + i_to, p_to)

    load_x = pltpu.make_async_copy(
        feat_ref, x_buf.at[a, pl.ds(pl.multiple_of(me * rows, rows), rows)], load_sem.at[0]
    )
    load_w = pltpu.make_async_copy(weight_ref, w_buf.at[i], load_sem.at[1])
    load_b = pltpu.make_async_copy(bias_ref, b_buf.at[i, 0], load_sem.at[2])
    load_h = pltpu.make_async_copy(head_ref, b_buf.at[i, 1], load_sem.at[3])
    load_x.start()
    load_w.start()
    load_b.start()
    load_h.start()

    barrier = pltpu.get_barrier_semaphore()
    others = outer * peers - 1

    def greet(k, _):
        at = lax.rem(a * peers + me + k, outer * peers)
        pl.semaphore_signal(
            barrier, inc=1, device_id=dev(at // peers, i, at % peers), device_id_type=MESH
        )
        return 0

    lax.fori_loop(1, others + 1, greet, 0)
    for k in range(1, inner):
        pl.semaphore_signal(
            barrier, inc=1, device_id=dev(a, lax.rem(i + k, inner), me), device_id_type=MESH
        )

    for t in range(towers):
        start = jnp.where(a == 0, hbias_ref[t], 0.0)
        for aa in range(outer):
            for pp in range(peers):
                part[aa, pp, pl.ds(t, 1)] = jnp.full((1, rows), start, jnp.float32)

    load_x.wait()
    load_w.wait()
    load_b.wait()
    load_h.wait()
    pl.semaphore_wait(barrier, others + inner - 1)

    def x_piece(aa, pp, h):
        return x_buf.at[aa, pl.ds(pl.multiple_of(pp * rows + h * piece, piece), piece)]

    def send_x(aa, pp, h, sem, to):
        ref = x_piece(aa, pp, h)
        return pltpu.make_async_remote_copy(
            src_ref=ref, dst_ref=ref, send_sem=sem, recv_sem=x_recv.at[aa, pp, h],
            device_id=to, device_id_type=MESH,
        )

    def up(aa, h):
        return send_x(aa, me, h, z_send.at[0, aa, h], dev(lax.rem(a + 1, outer), i, me))

    def down(aa, h):
        return send_x(aa, me, h, z_send.at[1, aa, h], dev(lax.rem(a + outer - 1, outer), i, me))

    def across(aa, k, h):
        to = dev(a, i, lax.rem(y + k, ys) * 2 + c)
        return send_x(aa, me, h, y_send.at[aa, k - 1, h], to)

    def sibling(aa, yy, h):
        return send_x(aa, yy * 2 + c, h, core_send.at[aa, yy, h], dev(a, i, partner))

    def arrived(aa, pp, h):
        send_x(aa, pp, h, z_send.at[0, aa, h], dev(a, i, partner)).wait_recv()

    def goes_up(aa):
        return (aa <= a) & (a + 1 < outer)

    def goes_down(aa):
        return (aa >= a) & (a > 0)

    def send_w(k, t):
        return pltpu.make_async_remote_copy(
            src_ref=w_buf.at[i, t], dst_ref=w_buf.at[i, t],
            send_sem=w_send.at[k - 1, t], recv_sem=w_recv.at[i, t],
            device_id=dev(a, lax.rem(i + k, inner), me), device_id_type=MESH,
        )

    def send_b(k):
        return pltpu.make_async_remote_copy(
            src_ref=b_buf.at[i], dst_ref=b_buf.at[i],
            send_sem=b_send.at[k - 1], recv_sem=b_recv.at[i],
            device_id=dev(a, lax.rem(i + k, inner), me), device_id_type=MESH,
        )

    def columns(ii):
        diagonal = lax.broadcasted_iota(jnp.int32, (hidden, hidden), 0) == (
            lax.broadcasted_iota(jnp.int32, (hidden, hidden), 1)
        )
        for w in range(2):
            both = b_buf[ii, w].astype(jnp.float32)
            for t in range(towers):
                picked = jnp.where(diagonal, both[t : t + 1], 0.0)
                column = jnp.sum(picked, axis=1, keepdims=True)
                c_buf[ii, w, t] = jnp.broadcast_to(column, (hidden, LANES))

    def nth(j):
        low = jnp.minimum(a, outer - 1 - a)
        near = jnp.where(j % 2 == 1, a - (j + 1) // 2, a + j // 2)
        far = jnp.where(a < outer - 1 - a, j, outer - 1 - j)
        return jnp.where(j <= 2 * low, near, far)

    def cross_first(aa, k, d):
        pp = lax.rem(y + k, ys) * 2 + c
        to = dev(lax.rem(a + outer + 1 - 2 * d, outer), i, me)
        return send_x(aa, pp, FIRST, f_send.at[d, aa, k - 1], to)

    def spread(aa, h, own):
        if not own:
            arrived(aa, me, h)
        pl.when(goes_up(aa))(lambda: up(aa, h).start())
        pl.when(goes_down(aa))(lambda: down(aa, h).start())
        if own or h != FIRST:
            for k in range(1, ys):
                across(aa, k, h).start()
        sibling(aa, y, h).start()

    def pass_on(aa, h):
        for k in range(1, ys):
            yy = lax.rem(y + k, ys)
            arrived(aa, yy * 2 + c, h)
            if h == FIRST:
                pl.when(goes_up(aa))(lambda k=k: cross_first(aa, k, 0).start())
                pl.when(goes_down(aa))(lambda k=k: cross_first(aa, k, 1).start())
            sibling(aa, yy, h).start()

    def settle(aa, yy):
        for h in range(pieces):
            arrived(aa, yy * 2 + (1 - c), h)

    span = 2 * rows
    cols = STEP_COLS if span % STEP_COLS == 0 else span

    def compute(aa, yy, ii, t0, t1):
        count = (t1 - t0) * hidden
        w = w_buf[ii, t0:t1].reshape(count, depth)
        bias = c_buf[ii, 0, t0:t1].reshape(count, LANES)
        head = c_buf[ii, 1, t0:t1].reshape(count, LANES)
        for n in range(span // cols):
            at = pl.ds(pl.multiple_of(yy * span + n * cols, LANES), cols)
            pre = lax.dot_general(
                w, x_buf[aa, at], (((1,), (1,)), ((), ())),
                preferred_element_type=jnp.float32,
            )
            for l in range(cols // LANES):
                tile = n * cols + l * LANES
                lane = pl.ds(tile % rows, LANES)
                v = jnp.maximum(pre[:, l * LANES : (l + 1) * LANES] + bias, 0.0) * head
                for t in range(t1 - t0):
                    total = jnp.sum(v[t * hidden : (t + 1) * hidden], axis=0, keepdims=True)
                    part[aa, yy * 2 + tile // rows, pl.ds(t0 + t, 1), lane] += total

    def send_part(aa, pp):
        return pltpu.make_async_remote_copy(
            src_ref=part.at[aa, pp], dst_ref=ret.at[a, me],
            send_sem=p_send.at[aa, pp], recv_sem=p_recv.at[a, me],
            device_id=dev(aa, i, pp), device_id_type=MESH,
        )

    def give_back(aa, yy):
        for cc in range(2):
            pp = yy * 2 + cc
            mine = (aa == a) & (pp == me)
            pl.when(jnp.logical_not(mine))(lambda pp=pp: send_part(aa, pp).start())

    def pair(u):
        return nth(u // ys), lax.rem(y + u % ys, ys)

    far = max(inner - 1, 1)
    half = towers // 2

    def own_jobs(u1):
        for u in range(done[0], u1):
            settle(*pair(u))

        def job(u, _):
            compute(*pair(u), i, 0, towers)
            return 0

        if u1 > done[0]:
            lax.fori_loop(done[0], u1, job, 0)
        done[0] = max(done[0], u1)

    def far_jobs(v0, v1, t0, t1):
        def job(q, _):
            compute(*pair(q // far), lax.rem(i + 1 + q % far, inner), t0, t1)
            return 0

        if v1 > v0 and inner > 1:
            lax.fori_loop(v0 * far, v1 * far, job, 0)
        if t1 == towers:
            for v in range(v0, v1):
                give_back(*pair(v))

    def low_jobs(v1):
        v1 = min(v1, done[0])
        far_jobs(done[1], v1, 0, half)
        done[1] = max(done[1], v1)

    def high_jobs(v1):
        v1 = min(v1, done[1])
        far_jobs(done[2], v1, half, towers)
        done[2] = max(done[2], v1)

    for h in range(pieces):
        spread(a, h, True)
    for k in range(1, inner):
        send_b(k).start()
        for t in range(towers):
            send_w(k, t).start()
    columns(i)

    def weights_arrived(part_of):
        if part_of in got:
            return
        got.add(part_of)
        for k in range(1, inner):
            ii = lax.rem(i + k, inner)
            if part_of == 0:
                pltpu.make_async_remote_copy(
                    src_ref=b_buf.at[ii], dst_ref=b_buf.at[ii], send_sem=b_send.at[0],
                    recv_sem=b_recv.at[ii], device_id=dev(a, ii, me), device_id_type=MESH,
                ).wait_recv()
                columns(ii)
            for t in range(half) if part_of == 0 else range(half, towers):
                pltpu.make_async_remote_copy(
                    src_ref=w_buf.at[ii, t], dst_ref=w_buf.at[ii, t], send_sem=w_send.at[0, t],
                    recv_sem=w_recv.at[ii, t], device_id=dev(a, ii, me), device_id_type=MESH,
                ).wait_recv()

    pairs = outer * ys
    done, got = [0, 0, 0], set()
    own_jobs(1)
    for j in range(1, outer):
        aa, before = nth(j), nth(j - 1)
        passed = 0
        window = pieces if j == 1 else max(1, pieces - 2)
        for h in range(pieces):
            spread(aa, h, False)
            upto = min(pieces, -(-pieces * (h + 1) // window))
            for g in range(passed, upto):
                pass_on(before, g)
            passed = upto
            if upto == pieces:
                own_jobs(j * ys)
            late = h >= window - 1
            if (j == outer - 2 and late) or j == outer - 1:
                weights_arrived(0)
                low_jobs(done[1] + 1)
            if j == outer - 1 and late:
                weights_arrived(1)
                high_jobs(done[2] + 2)
        if j < outer - 1:
            own_jobs(j * ys + 1)
    weights_arrived(0)
    weights_arrived(1)
    last = nth(outer - 1)
    for h in range(pieces - 2):
        pass_on(last, h)
    own_jobs((outer - 1) * ys + 1)
    for h in range(max(0, pieces - 2), pieces):
        pass_on(last, h)
    low_jobs(done[0])
    high_jobs(done[1])
    for u in range(done[0], pairs):
        own_jobs(u + 1)
        far_jobs(u, u + 1, 0, towers)

    def landed(aa, pp):
        pltpu.make_async_remote_copy(
            src_ref=part.at[aa, pp], dst_ref=ret.at[aa, pp], send_sem=p_send.at[aa, pp],
            recv_sem=p_recv.at[aa, pp], device_id=dev(a, i, partner), device_id_type=MESH,
        ).wait_recv()

    ret[a, me] = part[a, me]
    for aa in range(outer):
        for pp in range(peers):
            mine = (a == aa) & (me == pp)
            pl.when(jnp.logical_not(mine))(lambda aa=aa, pp=pp: landed(aa, pp))
    for pp in range(peers):
        total = ret[0, pp]
        for aa in range(1, outer):
            total += ret[aa, pp]
        out_ref[pp] = total

    for aa in range(outer):
        for h in range(pieces):
            pl.when(goes_up(aa))(lambda aa=aa, h=h: up(aa, h).wait_send())
            pl.when(goes_down(aa))(lambda aa=aa, h=h: down(aa, h).wait_send())
            for k in range(1, ys):
                sent = (a == aa) | (h != FIRST)
                pl.when(sent)(lambda aa=aa, k=k, h=h: across(aa, k, h).wait_send())
            for yy in range(ys):
                sibling(aa, yy, h).wait_send()
        for k in range(1, ys):
            pl.when(goes_up(aa))(lambda aa=aa, k=k: cross_first(aa, k, 0).wait_send())
            pl.when(goes_down(aa))(lambda aa=aa, k=k: cross_first(aa, k, 1).wait_send())
        for pp in range(peers):
            mine = (a == aa) & (me == pp)
            pl.when(jnp.logical_not(mine))(lambda aa=aa, pp=pp: send_part(aa, pp).wait_send())
    for k in range(1, inner):
        send_b(k).wait_send()
        for t in range(towers):
            send_w(k, t).wait_send()


def shards(features, task_mask, tower_in, tower_bias, tower_head, head_bias):
    peers, group = lax.axis_size("peer"), lax.axis_size("group")
    rows, depth = features.shape
    towers, hidden, _ = tower_in.shape
    inner = split_of_group(group, peers, tower_in.size, features.size)
    outer = group // inner
    ys = peers // 2
    pieces = rows // PIECE_ROWS
    dma = pltpu.SemaphoreType.DMA
    logits = pl.pallas_call(
        functools.partial(kernel, outer, inner, peers),
        out_shape=jax.ShapeDtypeStruct((peers, towers, rows), jnp.float32),
        in_specs=[pl.BlockSpec(memory_space=pl.ANY)] * 4
        + [pl.BlockSpec(memory_space=pltpu.SMEM)],
        out_specs=pl.BlockSpec(memory_space=pltpu.VMEM),
        scratch_shapes=[
            pltpu.VMEM((outer, peers * rows, depth), features.dtype),
            pltpu.VMEM((inner, towers, hidden, depth), tower_in.dtype),
            pltpu.VMEM((inner, 2, towers, hidden), tower_bias.dtype),
            pltpu.VMEM((inner, 2, towers, hidden, LANES), jnp.float32),
            pltpu.VMEM((outer, peers, towers, rows), jnp.float32),
            pltpu.VMEM((outer, peers, towers, rows), jnp.float32),
            dma((4,)),
            dma((outer, peers, pieces)),
            dma((2, outer, pieces)),
            dma((2, outer, max(1, ys - 1))),
            dma((outer, max(1, ys - 1), pieces)),
            dma((outer, ys, pieces)),
            dma((max(1, inner - 1), towers)),
            dma((inner, towers)),
            dma((max(1, inner - 1),)),
            dma((inner,)),
            dma((outer, peers)),
            dma((outer, peers)),
        ],
        compiler_params=pltpu.CompilerParams(
            collective_id=0, has_side_effects=True, vmem_limit_bytes=60 * 1024 * 1024
        ),
    )(features, tower_in, tower_bias, tower_head, head_bias)
    tasks = jnp.arange(peers * towers, dtype=jnp.int32)
    bits = (task_mask[:, None] >> tasks[None, :]) & 1
    return jnp.where(bits == 1, logits.reshape(peers * towers, rows).T, 0.0)


def solution(mesh):
    placed = (
        P(("group", "peer"), None),
        P(("group", "peer")),
        P("peer", "group", None),
        P("peer", "group"),
        P("peer", "group"),
        P("peer"),
    )
    return jax.shard_map(
        shards, mesh=mesh, in_specs=placed, out_specs=P(("group", "peer"), None), check_vma=False
    )
```

profile of v0, /device:TPU:0, one launch (start us, length us, event | category | flops | bytes accessed | tf_op | source)
XLA Modules:
  0.0 93.0 jit_solution(11223122420960892658)
XLA Ops:
  0.0 0.0 copy-start
  0.0 91.7 %shard_map.64 = f32[4,4,384]{2,1,0:T(4,128)} custom-call(bf16[384,1024]{1,0:T(8,128)(2,1)} %feat_ref.1, bf16[4,256,1024]{2,1,0:T(8,128)(2,1)} %weight_ref.1, bf16[4,256]{1,0:T(4,128)(2,1)} %bias_ref.1, bf16[4,256]{1,0:T(4,128)(2,1)} %head_ref.1, f32[4]{0:T(128)} %hbias_ref.1), custom_call_target="tpu_custom_call" | custom-call | tf_op jit(solution)/shard_map/pallas_call | solution.py:361
  91.7 0.8 reshape.4
  92.4 0.0 copy-done
  92.4 0.6 bitcast_select_fusion
Async XLA Ops:
  0.0 92.4 %copy-start = (s32[384]{0:T(512)S(1)}, s32[384]{0:T(512)}, u32[]{:S(2)}) copy-start(s32[384]{0:T(512)} %param.7) | copy-start | bytes 4612
where the time goes:
time: 93.3 us; the launch traced here: 93 us
  Pallas kernels  91.7 us (98%)
    pallas_call x1, Pallas kernels, shards(): pl.pallas_call(functools.partial(kernel, outer, inner, peers), out_shape=...  91.7 us

commit v1 on v0

v1 whole, which is shorter than its diff:
```python
import functools

import jax
import jax.numpy as jnp
from jax import lax
from jax.experimental import pallas as pl
from jax.experimental.pallas import tpu as pltpu
from jax.sharding import PartitionSpec as P

MESH = pl.DeviceIdType.MESH
LANES = 128
PIECE_ROWS = 64
LAG = 3
SLOT_TASKS = 14


def split_of_group(group, peers, weight_bytes, sample_bytes):
    sizes = [f for f in range(1, group + 1) if group % f == 0]

    def cost(f):
        return (f - 1) * weight_bytes + (group // f * peers - 1) * sample_bytes / 2

    return min(sizes, key=cost)


def crosses(outer, pieces, a, aa, h):
    if a == aa:
        return False
    ends = (aa == 0 and a == 1 or aa == outer - 1 and a == outer - 2) and 0 < a < outer - 1
    return ends or h == pieces - 1


def plan(outer, pieces):
    avail = [{(a, 0, h): 0 for h in range(pieces)} for a in range(outer)]
    sends = [{} for _ in range(outer)]
    arrivals = [{} for _ in range(outer)]
    done = set()
    slot = 0
    while any(len(have) < outer * pieces * 2 for have in avail):
        moves = []
        for a in range(outer):
            ends = a in (0, outer - 1)
            for way, to in ((0, a + 1), (1, a - 1)):
                if not 0 <= to < outer:
                    continue
                ready = [
                    (k, -abs(aa - a) if k else abs(aa - a), h, (aa, k, h))
                    for (aa, k, h), since in avail[a].items()
                    if since <= slot
                    and (a, way, aa, k, h) not in done
                    and (aa <= a if way == 0 else aa >= a)
                    and (k == 0 or crosses(outer, pieces, to, aa, h))
                ]
                if ready:
                    moves.append((a, way, to, min(ready)[-1]))
            ready = [
                (ends and abs(aa - a) == 1 and h == pieces - 2, since, abs(aa - a), h, (aa, 0, h))
                for (aa, k, h), since in avail[a].items()
                if since <= slot
                and k == 0
                and (a, 2, aa, k, h) not in done
                and not crosses(outer, pieces, a, aa, h)
            ]
            if ready:
                moves.append((a, 2, a, min(ready)[-1]))
        for a, way, to, (aa, k, h) in moves:
            done.add((a, way, aa, k, h))
            sends[a].setdefault((slot, way), (aa, k, h))
            got = (aa, 1 if way == 2 else k, h)
            avail[to][got] = slot + LAG
            arrivals[to].setdefault(slot, []).append(got)
        slot += 1
    return slot, sends, arrivals, avail


def tasks_of(outer, ys, pieces, towers, ready_far, avail):
    per = LANES // PIECE_ROWS
    orders = []
    for a in range(outer):
        groups = []
        for aa in range(outer):
            for k in range(ys):
                for q in range(pieces // per):
                    at = max(avail[a][aa, min(k, 1), h] for h in range(q * per, (q + 1) * per))
                    groups.append((max(at, 1), abs(aa - a), k, q, aa))
        orders.append(sorted(groups))
    count = len(orders[0])
    at = [max(orders[a][u][0] for a in range(outer)) for u in range(count)]
    at = [max(at[: u + 1]) for u in range(count)]
    last = at[-1]
    own = [[u for u in range(count) if at[u] == s] for s in range(last + 1)]
    far = []
    left = [(u, t) for t in range(towers) for u in range(count)]
    for s in range(last + 1):
        room = 10**6 if s == last else SLOT_TASKS - towers * len(own[s])
        now = [(u, t) for (u, t) in left if at[u] <= s and min(ready_far[t], last) <= s][: max(room, 0)]
        far.append(now)
        left = [x for x in left if x not in now]
    assert not left
    return [[(aa, k, q) for _, _, k, q, aa in order] for order in orders], own, far


def kernel(
    outer, inner, peers,
    feat_ref, weight_ref, bias_ref, head_ref, hbias_ref, out_ref,
    x_buf, w_buf, b_buf, c_buf, part, ret,
    load_x, load_sem, x_recv, z_send, y_send, core_send, w_send, w_recv, b_send, b_recv,
    p_send, p_recv,
):
    rows, depth = feat_ref.shape
    towers, hidden, _ = weight_ref.shape
    piece = PIECE_ROWS
    pieces = rows // piece
    per = LANES // piece
    quads = rows // LANES
    ys = peers // 2
    group_at, me = lax.axis_index("group"), lax.axis_index("peer")
    a, i = group_at // inner, group_at % inner
    y, c = me // 2, me % 2
    partner = y * 2 + (1 - c)

    def dev(a_to, i_to, p_to):
        return (a_to * inner + i_to, p_to)

    def sel(values):
        out = values[-1]
        for at in range(outer - 2, -1, -1):
            if not isinstance(out, int) or values[at] != out:
                out = jnp.where(a == at, values[at], out)
        return out

    def when(flags, do):
        if all(flags):
            do()
        elif any(flags):
            pl.when(sel([int(f) for f in flags]) == 1)(do)

    loads = [
        pltpu.make_async_copy(
            feat_ref.at[pl.ds(q * LANES, LANES)], x_buf.at[a, y, q, c], load_x.at[q]
        )
        for q in range(quads)
    ]
    load_w = pltpu.make_async_copy(weight_ref, w_buf.at[i], load_sem.at[0])
    load_b = pltpu.make_async_copy(bias_ref, b_buf.at[i, 0], load_sem.at[1])
    load_h = pltpu.make_async_copy(head_ref, b_buf.at[i, 1], load_sem.at[2])
    for load in loads:
        load.start()
    load_w.start()
    load_b.start()
    load_h.start()

    barrier = pltpu.get_barrier_semaphore()

    def greet(to):
        pl.semaphore_signal(barrier, inc=1, device_id=to, device_id_type=MESH)

    pl.when(a + 1 < outer)(lambda: greet(dev(lax.rem(a + 1, outer), i, me)))
    pl.when(a > 0)(lambda: greet(dev(lax.rem(a + outer - 1, outer), i, me)))
    for k in range(1, ys):
        greet(dev(a, i, lax.rem(y + k, ys) * 2 + c))
    for k in range(1, inner):
        greet(dev(a, lax.rem(i + k, inner), me))
    greet(dev(a, i, partner))
    neighbours = sel([(at > 0) + (at + 1 < outer) + ys + inner - 1 for at in range(outer)])

    def column(k):
        return lax.rem(y + k, ys) if k else y

    def send_x(aa, yy, cc, h, sem, to):
        ref = x_buf.at[aa, yy, h // per, cc, pl.ds(pl.multiple_of(h % per * piece, piece), piece)]
        return pltpu.make_async_remote_copy(
            src_ref=ref, dst_ref=ref, send_sem=sem, recv_sem=x_recv.at[aa, yy * 2 + cc, h],
            device_id=to, device_id_type=MESH,
        )

    def along(way, aa, k, h):
        to = lax.rem(a + 1, outer) if way == 0 else lax.rem(a + outer - 1, outer)
        return send_x(aa, column(k), c, h, z_send.at[way, aa, k, h], dev(to, i, me))

    def across(aa, k, h):
        to = dev(a, i, lax.rem(y + k, ys) * 2 + c)
        return send_x(aa, y, c, h, y_send.at[aa, k - 1, h], to)

    def sibling(aa, k, h):
        return send_x(aa, column(k), c, h, core_send.at[aa, k, h], dev(a, i, partner))

    def arrived(aa, k, cc, h):
        send_x(aa, column(k), cc, h, core_send.at[aa, k, h], dev(a, i, partner)).wait_recv()

    def send_w(k, t):
        return pltpu.make_async_remote_copy(
            src_ref=w_buf.at[i, t], dst_ref=w_buf.at[i, t],
            send_sem=w_send.at[k - 1, t], recv_sem=w_recv.at[i, t],
            device_id=dev(a, lax.rem(i + k, inner), me), device_id_type=MESH,
        )

    def send_b(k):
        return pltpu.make_async_remote_copy(
            src_ref=b_buf.at[i], dst_ref=b_buf.at[i],
            send_sem=b_send.at[k - 1], recv_sem=b_recv.at[i],
            device_id=dev(a, lax.rem(i + k, inner), me), device_id_type=MESH,
        )

    def columns(ii):
        diagonal = lax.broadcasted_iota(jnp.int32, (hidden, hidden), 0) == (
            lax.broadcasted_iota(jnp.int32, (hidden, hidden), 1)
        )
        for w in range(2):
            both = b_buf[ii, w].astype(jnp.float32)
            for t in range(towers):
                picked = jnp.where(diagonal, both[t : t + 1], 0.0)
                total = jnp.sum(picked, axis=1, keepdims=True)
                c_buf[ii, w, t] = jnp.broadcast_to(total, (hidden, LANES))

    def compute(group, ii, t, first):
        aa, yy, q = group
        x = x_buf[aa, yy, q].reshape(2 * LANES, depth)
        pre = lax.dot_general(
            w_buf[ii, t], x, (((1,), (1,)), ((), ())), preferred_element_type=jnp.float32
        )
        bias, head = c_buf[ii, 0, t], c_buf[ii, 1, t]
        lanes = pl.ds(pl.multiple_of(q * LANES, LANES), LANES)
        for cc in range(2):
            v = jnp.maximum(pre[:, cc * LANES : (cc + 1) * LANES] + bias, 0.0) * head
            total = jnp.sum(v, axis=0, keepdims=True)
            if first:
                total += jnp.where(a == 0, hbias_ref[t], 0.0)
            else:
                total += part[aa, yy * 2 + cc, pl.ds(t, 1), lanes]
            part[aa, yy * 2 + cc, pl.ds(t, 1), lanes] = total

    def send_part(aa, pp):
        return pltpu.make_async_remote_copy(
            src_ref=part.at[aa, pp], dst_ref=ret.at[a, me],
            send_sem=p_send.at[aa, pp], recv_sem=p_recv.at[a, me],
            device_id=dev(aa, i, pp), device_id_type=MESH,
        )

    def give_back(aa, yy):
        for cc in range(2):
            pp = yy * 2 + cc
            mine = (aa == a) & (pp == me)
            pl.when(jnp.logical_not(mine))(lambda pp=pp: send_part(aa, pp).start())

    slots, sends, arrivals, avail = plan(outer, pieces)
    ready_far = [-(-hidden * max(inner - 1, 1) * (t + 1) // piece) + 2 for t in range(towers)]
    orders, own, far = tasks_of(outer, ys, pieces, towers, ready_far, avail)
    steps = len(own)
    settled = [set() for _ in range(outer)]
    done_at = {}
    for s in range(steps):
        for u in own[s]:
            done_at[u] = s
        for u, _ in far[s]:
            done_at[u] = s

    def group_of(u):
        aa = sel([orders[at][u][0] for at in range(outer)])
        k = sel([orders[at][u][1] for at in range(outer)])
        q = sel([orders[at][u][2] for at in range(outer)])
        return aa, (lax.rem(y + k, ys) if not isinstance(k, int) or k else y), q

    def start_sends(slot):
        for way in range(3):
            entries = [sends[at].get((slot, way)) for at in range(outer)]
            flags = [e is not None for e in entries]
            if not any(flags):
                continue
            some = next(e for e in entries if e is not None)
            entries = [e or some for e in entries]
            issue_sends(way, entries, flags, True)

    def issue_sends(way, entries, flags, start):
        aa = sel([e[0] for e in entries])
        h = sel([e[2] for e in entries])
        kinds = sorted({e[1] for e, f in zip(entries, flags) if f})

        for kind in kinds:

            def go(kind=kind):
                for k in range(1, ys) if way == 2 or kind else (0,):
                    copy = across(aa, k, h) if way == 2 else along(way, aa, k, h)
                    copy.start() if start else copy.wait_send()

            when([f and e[1] == kind for e, f in zip(entries, flags)], go)

    def take(slot):
        lists = [arrivals[at].get(slot, []) for at in range(outer)]
        for n in range(max(len(x) for x in lists)):
            for kind in range(2):
                flags = [len(x) > n and x[n][1] == kind for x in lists]
                if not any(flags):
                    continue
                some = next(x[n] for x, f in zip(lists, flags) if f)
                entries = [x[n] if f else some for x, f in zip(lists, flags)]
                aa = sel([e[0] for e in entries])
                h = sel([e[2] for e in entries])

                def relay(aa=aa, h=h, kind=kind):
                    for k in range(1, ys) if kind else (0,):
                        arrived(aa, k, c, h)
                        sibling(aa, k, h).start()

                when(flags, relay)

    def settle(u):
        aa = sel([orders[at][u][0] for at in range(outer)])
        k = sel([orders[at][u][1] for at in range(outer)])
        q = sel([orders[at][u][2] for at in range(outer)])
        yy = lax.rem(y + k, ys)
        for n in range(per):
            ref = x_buf.at[aa, yy, q, 1 - c, pl.ds(n * piece, piece)]
            pltpu.make_async_remote_copy(
                src_ref=ref, dst_ref=ref, send_sem=core_send.at[aa, k, q * per + n],
                recv_sem=x_recv.at[aa, yy * 2 + 1 - c, q * per + n],
                device_id=dev(a, i, partner), device_id_type=MESH,
            ).wait_recv()

    def weights_arrived(t):
        for k in range(1, inner):
            ii = lax.rem(i + k, inner)
            pltpu.make_async_remote_copy(
                src_ref=w_buf.at[ii, t], dst_ref=w_buf.at[ii, t], send_sem=w_send.at[0, t],
                recv_sem=w_recv.at[ii, t], device_id=dev(a, ii, me), device_id_type=MESH,
            ).wait_recv()

    def biases_arrived():
        for k in range(1, inner):
            ii = lax.rem(i + k, inner)
            pltpu.make_async_remote_copy(
                src_ref=b_buf.at[ii], dst_ref=b_buf.at[ii], send_sem=b_send.at[0],
                recv_sem=b_recv.at[ii], device_id=dev(a, ii, me), device_id_type=MESH,
            ).wait_recv()
            columns(ii)

    pl.semaphore_wait(barrier, neighbours)
    for q, load in enumerate(loads):
        load.wait()
        if q == 0:
            start_sends(0)
            start_sends(1)
        for h in range(q * per, (q + 1) * per):
            sibling(a, 0, h).start()
    load_b.wait()
    load_h.wait()
    for k in range(1, inner):
        send_b(k).start()
    load_w.wait()
    for t in range(towers):
        for k in range(1, inner):
            send_w(k, t).start()
    columns(i)

    weights = set()
    for s in range(1, steps):
        take(s - 2)
        start_sends(s + 1)
        if s == 2:
            biases_arrived()
        for u in own[s]:
            settle(u)
            group = group_of(u)
            for t in range(towers):
                compute(group, i, t, True)
        for u, t in far[s]:
            if t not in weights:
                weights.add(t)
                weights_arrived(t)
            group = group_of(u)
            if inner == 2:
                compute(group, lax.rem(i + 1, inner), t, False)
            elif inner > 2:

                def each(k, _, group=group, t=t):
                    compute(group, lax.rem(i + k, inner), t, False)
                    return 0

                lax.fori_loop(1, inner, each, 0)
        ended = []
        for at in range(outer):
            pairs = {}
            for u, (aa, k, q) in enumerate(orders[at]):
                pairs.setdefault((aa, k), []).append(done_at[u])
            ended.append(sorted(p for p, when_done in pairs.items() if max(when_done) == s))
        for n in range(max(len(x) for x in ended)):
            flags = [len(x) > n for x in ended]
            some = next(x[n] for x in ended if len(x) > n)
            entries = [x[n] if len(x) > n else some for x in ended]
            aa = sel([e[0] for e in entries])
            k = sel([e[1] for e in entries])
            when(flags, lambda: give_back(aa, lax.rem(y + k, ys)))

    def landed(aa, pp):
        pltpu.make_async_remote_copy(
            src_ref=part.at[aa, pp], dst_ref=ret.at[aa, pp], send_sem=p_send.at[aa, pp],
            recv_sem=p_recv.at[aa, pp], device_id=dev(a, i, partner), device_id_type=MESH,
        ).wait_recv()

    for slot in range(slots):
        for way in range(3):
            entries = [sends[at].get((slot, way)) for at in range(outer)]
            flags = [e is not None for e in entries]
            if any(flags):
                some = next(e for e in entries if e is not None)
                issue_sends(way, [e or some for e in entries], flags, False)
    for aa in range(outer):
        for k in range(ys):
            for h in range(pieces):
                sibling(aa, k, h).wait_send()
    for k in range(1, inner):
        send_b(k).wait_send()
        for t in range(towers):
            send_w(k, t).wait_send()

    ret[a, me] = part[a, me]
    for aa in range(outer):
        for pp in range(peers):
            mine = (a == aa) & (me == pp)
            pl.when(jnp.logical_not(mine))(lambda aa=aa, pp=pp: landed(aa, pp))
    for pp in range(peers):
        total = ret[0, pp]
        for aa in range(1, outer):
            total += ret[aa, pp]
        out_ref[pp * towers : (pp + 1) * towers] = total
    for aa in range(outer):
        for pp in range(peers):
            mine = (a == aa) & (me == pp)
            pl.when(jnp.logical_not(mine))(lambda aa=aa, pp=pp: send_part(aa, pp).wait_send())


def shards(features, task_mask, tower_in, tower_bias, tower_head, head_bias):
    peers, group = lax.axis_size("peer"), lax.axis_size("group")
    rows, depth = features.shape
    towers, hidden, _ = tower_in.shape
    inner = split_of_group(group, peers, tower_in.size, features.size)
    outer = group // inner
    ys = peers // 2
    pieces = rows // PIECE_ROWS
    dma = pltpu.SemaphoreType.DMA
    logits = pl.pallas_call(
        functools.partial(kernel, outer, inner, peers),
        out_shape=jax.ShapeDtypeStruct((peers * towers, rows), jnp.float32),
        in_specs=[pl.BlockSpec(memory_space=pl.ANY)] * 4
        + [pl.BlockSpec(memory_space=pltpu.SMEM)],
        out_specs=pl.BlockSpec(memory_space=pltpu.VMEM),
        scratch_shapes=[
            pltpu.VMEM((outer, ys, rows // LANES, 2, LANES, depth), features.dtype),
            pltpu.VMEM((inner, towers, hidden, depth), tower_in.dtype),
            pltpu.VMEM((inner, 2, towers, hidden), tower_bias.dtype),
            pltpu.VMEM((inner, 2, towers, hidden, LANES), jnp.float32),
            pltpu.VMEM((outer, peers, towers, rows), jnp.float32),
            pltpu.VMEM((outer, peers, towers, rows), jnp.float32),
            dma((rows // LANES,)),
            dma((3,)),
            dma((outer, peers, pieces)),
            dma((2, outer, ys, pieces)),
            dma((outer, max(1, ys - 1), pieces)),
            dma((outer, ys, pieces)),
            dma((max(1, inner - 1), towers)),
            dma((inner, towers)),
            dma((max(1, inner - 1),)),
            dma((inner,)),
            dma((outer, peers)),
            dma((outer, peers)),
        ],
        compiler_params=pltpu.CompilerParams(
            collective_id=0, has_side_effects=True, vmem_limit_bytes=60 * 1024 * 1024
        ),
    )(features, tower_in, tower_bias, tower_head, head_bias)
    tasks = jnp.arange(peers * towers, dtype=jnp.int32)
    bits = (task_mask[:, None] >> tasks[None, :]) & 1
    return jnp.where(bits == 1, logits.T, 0.0)


def solution(mesh):
    placed = (
        P(("group", "peer"), None),
        P(("group", "peer")),
        P("peer", "group", None),
        P("peer", "group"),
        P("peer", "group"),
        P("peer"),
    )
    return jax.shard_map(
        shards, mesh=mesh, in_specs=placed, out_specs=P(("group", "peer"), None), check_vma=False
    )
```

time: 93.3 us -> 79.8 us (0.86)
  Pallas kernels: 91.7 us -> 78.2 us
    pallas_call x1, Pallas kernels: 91.7 us -> 78.2 us  [shards(): pl.pallas_call(functools.partial(kernel, outer, inner, peers), out_shape=...]
where the time goes in v1:
time: 79.8 us; the launch traced here: 79.6 us
  Pallas kernels  78.2 us (98%)
  other arithmetic  1.35 us (2%)
    pallas_call x1, Pallas kernels, shards(): pl.pallas_call(functools.partial(kernel, outer, inner, peers), out_shape=...  78.2 us

profile of v1, /device:TPU:0, one launch (start us, length us, event | category | flops | bytes accessed | tf_op | source)
XLA Modules:
  0.0 79.6 jit_solution(9445589636747411704)
XLA Ops:
  0.0 0.0 copy-start
  0.0 78.2 %shard_map.64 = f32[16,384]{1,0:T(8,128)} custom-call(bf16[384,1024]{1,0:T(8,128)(2,1)} %feat_ref.1, bf16[4,256,1024]{2,1,0:T(8,128)(2,1)} %weight_ref.1, bf16[4,256]{1,0:T(4,128)(2,1)} %bias_ref.1, bf16[4,256]{1,0:T(4,128)(2,1)} %head_ref.1, f32[4]{0:T(128)} %hbias_ref.1), custom_call_target="tpu_custom_call" | custom-call | tf_op jit(solution)/shard_map/pallas_call | solution.py:441
  78.2 0.0 copy-done
  78.2 1.4 %bitcast_select_fusion = f32[384,16]{0,1:T(8,128)} fusion(f32[16,384]{1,0:T(8,128)} %shard_map.64, s32[384]{0:T(512)S(1)} %copy-done), kind=kLoop, calls=%fused_computation | loop fusion | flops 24576 | bytes 50688 | tf_op jit(solution)/shard_map/jit(_where)/select_n | solution.py:473
Async XLA Ops:
  0.0 78.2 %copy-start = (s32[384]{0:T(512)S(1)}, s32[384]{0:T(512)}, u32[]{:S(2)}) copy-start(s32[384]{0:T(512)} %param.7) | copy-start | bytes 4612

commit v2 on v1

--- a/solution.py
+++ b/solution.py
@@ -44,7 +44,7 @@
                 if not 0 <= to < outer:
                     continue
                 ready = [
-                    (k, -abs(aa - a) if k else abs(aa - a), h, (aa, k, h))
+                    (k, k and abs(aa - to) == 1, abs(aa - to), h, (aa, k, h))
                     for (aa, k, h), since in avail[a].items()
                     if since <= slot
                     and (a, way, aa, k, h) not in done
@@ -68,7 +68,7 @@
             sends[a].setdefault((slot, way), (aa, k, h))
             got = (aa, 1 if way == 2 else k, h)
             avail[to][got] = slot + LAG
-            arrivals[to].setdefault(slot, []).append(got)
+            arrivals[to].setdefault(slot, []).append((*got, way))
         slot += 1
     return slot, sends, arrivals, avail
 
@@ -104,8 +104,7 @@
     outer, inner, peers,
     feat_ref, weight_ref, bias_ref, head_ref, hbias_ref, out_ref,
     x_buf, w_buf, b_buf, c_buf, part, ret,
-    load_x, load_sem, x_recv, z_send, y_send, core_send, w_send, w_recv, b_send, b_recv,
-    p_send, p_recv,
+    load_sem, x_recv, core_recv, x_send, core_send, w_send, w_recv, b_send, b_recv, p_send, p_recv,
 ):
     rows, depth = feat_ref.shape
     towers, hidden, _ = weight_ref.shape
@@ -135,15 +134,22 @@
         elif any(flags):
             pl.when(sel([int(f) for f in flags]) == 1)(do)
 
+    def at_group(aa, yy, q):
+        return (aa * ys + yy) * quads + q
+
+    def x_rows(aa, yy, q, cc, start=0, size=LANES):
+        row = (at_group(aa, yy, q) * 2 + cc) * LANES + start
+        return x_buf.at[pl.ds(pl.multiple_of(row, PIECE_ROWS), size)]
+
     loads = [
         pltpu.make_async_copy(
-            feat_ref.at[pl.ds(q * LANES, LANES)], x_buf.at[a, y, q, c], load_x.at[q]
+            feat_ref.at[pl.ds(q * LANES, LANES)], x_rows(a, y, q, c), load_sem.at[q]
         )
         for q in range(quads)
     ]
-    load_w = pltpu.make_async_copy(weight_ref, w_buf.at[i], load_sem.at[0])
-    load_b = pltpu.make_async_copy(bias_ref, b_buf.at[i, 0], load_sem.at[1])
-    load_h = pltpu.make_async_copy(head_ref, b_buf.at[i, 1], load_sem.at[2])
+    load_w = pltpu.make_async_copy(weight_ref, w_buf.at[i], load_sem.at[quads])
+    load_b = pltpu.make_async_copy(bias_ref, b_buf.at[i, 0], load_sem.at[quads + 1])
+    load_h = pltpu.make_async_copy(head_ref, b_buf.at[i, 1], load_sem.at[quads + 2])
     for load in loads:
         load.start()
     load_w.start()
@@ -167,40 +173,57 @@
     def column(k):
         return lax.rem(y + k, ys) if k else y
 
-    def send_x(aa, yy, cc, h, sem, to):
-        ref = x_buf.at[aa, yy, h // per, cc, pl.ds(pl.multiple_of(h % per * piece, piece), piece)]
+    def send_x(aa, yy, h, send_sem, recv_sem, to):
+        ref = x_rows(aa, yy, h // per, c, h % per * piece, piece)
         return pltpu.make_async_remote_copy(
-            src_ref=ref, dst_ref=ref, send_sem=sem, recv_sem=x_recv.at[aa, yy * 2 + cc, h],
+            src_ref=ref, dst_ref=ref, send_sem=send_sem, recv_sem=recv_sem,
             device_id=to, device_id_type=MESH,
         )
 
-    def along(way, aa, k, h):
+    def along(way, aa, k, h, slot):
         to = lax.rem(a + 1, outer) if way == 0 else lax.rem(a + outer - 1, outer)
-        return send_x(aa, column(k), c, h, z_send.at[way, aa, k, h], dev(to, i, me))
-
-    def across(aa, k, h):
+        return send_x(aa, column(k), h, x_send.at[0], x_recv.at[0, slot], dev(to, i, me))
+
+    def across(aa, k, h, slot):
         to = dev(a, i, lax.rem(y + k, ys) * 2 + c)
-        return send_x(aa, y, c, h, y_send.at[aa, k - 1, h], to)
+        return send_x(aa, y, h, x_send.at[0], x_recv.at[1, slot], to)
 
     def sibling(aa, k, h):
-        return send_x(aa, column(k), c, h, core_send.at[aa, k, h], dev(a, i, partner))
-
-    def arrived(aa, k, cc, h):
-        send_x(aa, column(k), cc, h, core_send.at[aa, k, h], dev(a, i, partner)).wait_recv()
+        sem = core_recv.at[at_group(aa, column(k), h // per)]
+        return send_x(aa, column(k), h, core_send.at[0], sem, dev(a, i, partner))
+
+    def await_rows(count, sem):
+        ref = x_buf.at[pl.ds(0, count)]
+        pltpu.make_async_remote_copy(
+            src_ref=ref, dst_ref=ref, send_sem=x_send.at[0], recv_sem=sem,
+            device_id=dev(a, i, partner), device_id_type=MESH,
+        ).wait_recv()
+
+    def await_sent(count, sem):
+        ref = x_buf.at[pl.ds(0, count)]
+        pltpu.make_async_remote_copy(
+            src_ref=ref, dst_ref=ref, send_sem=sem.at[0], recv_sem=p_recv.at[0],
+            device_id=dev(a, i, partner), device_id_type=MESH,
+        ).wait_send()
 
     def send_w(k, t):
         return pltpu.make_async_remote_copy(
-            src_ref=w_buf.at[i, t], dst_ref=w_buf.at[i, t],
-            send_sem=w_send.at[k - 1, t], recv_sem=w_recv.at[i, t],
-            device_id=dev(a, lax.rem(i + k, inner), me), device_id_type=MESH,
+            src_ref=w_buf.at[i, t], dst_ref=w_buf.at[i, t], send_sem=w_send.at[0],
+            recv_sem=w_recv.at[t], device_id=dev(a, lax.rem(i + k, inner), me), device_id_type=MESH,
         )
 
     def send_b(k):
         return pltpu.make_async_remote_copy(
-            src_ref=b_buf.at[i], dst_ref=b_buf.at[i],
-            send_sem=b_send.at[k - 1], recv_sem=b_recv.at[i],
-            device_id=dev(a, lax.rem(i + k, inner), me), device_id_type=MESH,
-        )
+            src_ref=b_buf.at[i], dst_ref=b_buf.at[i], send_sem=b_send.at[0],
+            recv_sem=b_recv.at[0], device_id=dev(a, lax.rem(i + k, inner), me), device_id_type=MESH,
+        )
+
+    def await_all(ref, send_sem, recv_sem, sent):
+        copy = pltpu.make_async_remote_copy(
+            src_ref=ref, dst_ref=ref, send_sem=send_sem.at[0], recv_sem=recv_sem,
+            device_id=dev(a, i, partner), device_id_type=MESH,
+        )
+        copy.wait_send() if sent else copy.wait_recv()
 
     def columns(ii):
         diagonal = lax.broadcasted_iota(jnp.int32, (hidden, hidden), 0) == (
@@ -215,7 +238,8 @@
 
     def compute(group, ii, t, first):
         aa, yy, q = group
-        x = x_buf[aa, yy, q].reshape(2 * LANES, depth)
+        row = pl.multiple_of(at_group(aa, yy, q) * 2 * LANES, 2 * LANES)
+        x = x_buf[pl.ds(row, 2 * LANES)]
         pre = lax.dot_general(
             w_buf[ii, t], x, (((1,), (1,)), ((), ())), preferred_element_type=jnp.float32
         )
@@ -227,13 +251,13 @@
             if first:
                 total += jnp.where(a == 0, hbias_ref[t], 0.0)
             else:
-                total += part[aa, yy * 2 + cc, pl.ds(t, 1), lanes]
-            part[aa, yy * 2 + cc, pl.ds(t, 1), lanes] = total
+                total += part[aa * peers + yy * 2 + cc, pl.ds(t, 1), lanes]
+            part[aa * peers + yy * 2 + cc, pl.ds(t, 1), lanes] = total
 
     def send_part(aa, pp):
         return pltpu.make_async_remote_copy(
-            src_ref=part.at[aa, pp], dst_ref=ret.at[a, me],
-            send_sem=p_send.at[aa, pp], recv_sem=p_recv.at[a, me],
+            src_ref=part.at[aa * peers + pp], dst_ref=ret.at[a * peers + me],
+            send_sem=p_send.at[0], recv_sem=p_recv.at[0],
             device_id=dev(aa, i, pp), device_id_type=MESH,
         )
 
@@ -247,7 +271,6 @@
     ready_far = [-(-hidden * max(inner - 1, 1) * (t + 1) // piece) + 2 for t in range(towers)]
     orders, own, far = tasks_of(outer, ys, pieces, towers, ready_far, avail)
     steps = len(own)
-    settled = [set() for _ in range(outer)]
     done_at = {}
     for s in range(steps):
         for u in own[s]:
@@ -269,9 +292,9 @@
                 continue
             some = next(e for e in entries if e is not None)
             entries = [e or some for e in entries]
-            issue_sends(way, entries, flags, True)
-
-    def issue_sends(way, entries, flags, start):
+            issue_sends(way, entries, flags, slot)
+
+    def issue_sends(way, entries, flags, slot):
         aa = sel([e[0] for e in entries])
         h = sel([e[2] for e in entries])
         kinds = sorted({e[1] for e, f in zip(entries, flags) if f})
@@ -280,68 +303,55 @@
 
             def go(kind=kind):
                 for k in range(1, ys) if way == 2 or kind else (0,):
-                    copy = across(aa, k, h) if way == 2 else along(way, aa, k, h)
-                    copy.start() if start else copy.wait_send()
+                    copy = across(aa, k, h, slot) if way == 2 else along(way, aa, k, h, slot)
+                    copy.start()
 
             when([f and e[1] == kind for e, f in zip(entries, flags)], go)
+
+    def by_count(counts, do):
+        for count in sorted(set(counts) - {0}):
+            when([n == count for n in counts], lambda count=count: do(count))
 
     def take(slot):
         lists = [arrivals[at].get(slot, []) for at in range(outer)]
-        for n in range(max(len(x) for x in lists)):
-            for kind in range(2):
-                flags = [len(x) > n and x[n][1] == kind for x in lists]
-                if not any(flags):
-                    continue
-                some = next(x[n] for x, f in zip(lists, flags) if f)
-                entries = [x[n] if f else some for x, f in zip(lists, flags)]
-                aa = sel([e[0] for e in entries])
-                h = sel([e[2] for e in entries])
-
-                def relay(aa=aa, h=h, kind=kind):
-                    for k in range(1, ys) if kind else (0,):
-                        arrived(aa, k, c, h)
-                        sibling(aa, k, h).start()
-
-                when(flags, relay)
+        for link in range(2):
+            kept = [[e for *e, way in x if (way == 2) == (link == 1)] for x in lists]
+            counts = [sum(ys - 1 if k else 1 for _, k, _ in x) for x in kept]
+            by_count(counts, lambda n: await_rows(n * piece, x_recv.at[link, slot]))
+            for n in range(max(len(x) for x in kept)):
+                for kind in range(2):
+                    flags = [len(x) > n and x[n][1] == kind for x in kept]
+                    if not any(flags):
+                        continue
+                    some = next(x[n] for x, f in zip(kept, flags) if f)
+                    entries = [x[n] if f else some for x, f in zip(kept, flags)]
+                    aa = sel([e[0] for e in entries])
+                    h = sel([e[2] for e in entries])
+
+                    def relay(aa=aa, h=h, kind=kind):
+                        for k in range(1, ys) if kind else (0,):
+                            sibling(aa, k, h).start()
+
+                    when(flags, relay)
 
     def settle(u):
-        aa = sel([orders[at][u][0] for at in range(outer)])
-        k = sel([orders[at][u][1] for at in range(outer)])
-        q = sel([orders[at][u][2] for at in range(outer)])
-        yy = lax.rem(y + k, ys)
-        for n in range(per):
-            ref = x_buf.at[aa, yy, q, 1 - c, pl.ds(n * piece, piece)]
-            pltpu.make_async_remote_copy(
-                src_ref=ref, dst_ref=ref, send_sem=core_send.at[aa, k, q * per + n],
-                recv_sem=x_recv.at[aa, yy * 2 + 1 - c, q * per + n],
-                device_id=dev(a, i, partner), device_id_type=MESH,
-            ).wait_recv()
+        await_rows(LANES, core_recv.at[at_group(*group_of(u))])
 
     def weights_arrived(t):
+        if inner > 1:
+            await_all(w_buf.at[pl.ds(0, inner - 1), t], w_send, w_recv.at[t], False)
+
+    def biases_arrived():
+        if inner > 1:
+            await_all(b_buf.at[pl.ds(0, inner - 1)], b_send, b_recv.at[0], False)
         for k in range(1, inner):
-            ii = lax.rem(i + k, inner)
-            pltpu.make_async_remote_copy(
-                src_ref=w_buf.at[ii, t], dst_ref=w_buf.at[ii, t], send_sem=w_send.at[0, t],
-                recv_sem=w_recv.at[ii, t], device_id=dev(a, ii, me), device_id_type=MESH,
-            ).wait_recv()
-
-    def biases_arrived():
-        for k in range(1, inner):
-            ii = lax.rem(i + k, inner)
-            pltpu.make_async_remote_copy(
-                src_ref=b_buf.at[ii], dst_ref=b_buf.at[ii], send_sem=b_send.at[0],
-                recv_sem=b_recv.at[ii], device_id=dev(a, ii, me), device_id_type=MESH,
-            ).wait_recv()
-            columns(ii)
+            columns(lax.rem(i + k, inner))
 
     pl.semaphore_wait(barrier, neighbours)
-    for q, load in enumerate(loads):
+    for load in loads:
         load.wait()
-        if q == 0:
-            start_sends(0)
-            start_sends(1)
-        for h in range(q * per, (q + 1) * per):
-            sibling(a, 0, h).start()
+    start_sends(0)
+    start_sends(1)
     load_b.wait()
     load_h.wait()
     for k in range(1, inner):
@@ -351,18 +361,11 @@
         for k in range(1, inner):
             send_w(k, t).start()
     columns(i)
+    for h in range(pieces):
+        sibling(a, 0, h).start()
 
     weights = set()
-    for s in range(1, steps):
-        take(s - 2)
-        start_sends(s + 1)
-        if s == 2:
-            biases_arrived()
-        for u in own[s]:
-            settle(u)
-            group = group_of(u)
-            for t in range(towers):
-                compute(group, i, t, True)
+    def far_tasks(s):
         for u, t in far[s]:
             if t not in weights:
                 weights.add(t)
@@ -377,6 +380,20 @@
                     return 0
 
                 lax.fori_loop(1, inner, each, 0)
+
+    for s in range(1, steps):
+        for u in own[s]:
+            settle(u)
+            for t in range(towers):
+                compute(group_of(u), i, t, True)
+        if s > slots:
+            far_tasks(s)
+        take(s - 2)
+        start_sends(s + 1)
+        if s == 2:
+            biases_arrived()
+        if s <= slots:
+            far_tasks(s)
         ended = []
         for at in range(outer):
             pairs = {}
@@ -391,42 +408,23 @@
             k = sel([e[1] for e in entries])
             when(flags, lambda: give_back(aa, lax.rem(y + k, ys)))
 
-    def landed(aa, pp):
-        pltpu.make_async_remote_copy(
-            src_ref=part.at[aa, pp], dst_ref=ret.at[aa, pp], send_sem=p_send.at[aa, pp],
-            recv_sem=p_recv.at[aa, pp], device_id=dev(a, i, partner), device_id_type=MESH,
-        ).wait_recv()
-
-    for slot in range(slots):
-        for way in range(3):
-            entries = [sends[at].get((slot, way)) for at in range(outer)]
-            flags = [e is not None for e in entries]
-            if any(flags):
-                some = next(e for e in entries if e is not None)
-                issue_sends(way, [e or some for e in entries], flags, False)
-    for aa in range(outer):
-        for k in range(ys):
-            for h in range(pieces):
-                sibling(aa, k, h).wait_send()
-    for k in range(1, inner):
-        send_b(k).wait_send()
-        for t in range(towers):
-            send_w(k, t).wait_send()
-
-    ret[a, me] = part[a, me]
-    for aa in range(outer):
-        for pp in range(peers):
-            mine = (a == aa) & (me == pp)
-            pl.when(jnp.logical_not(mine))(lambda aa=aa, pp=pp: landed(aa, pp))
+    counts = []
+    for at in range(outer):
+        each_way = [(ys - 1 if way == 2 or e[1] else 1) for (_, way), e in sends[at].items()]
+        counts.append(sum(each_way))
+    by_count(counts, lambda n: await_sent(n * piece, x_send))
+    await_sent(outer * ys * pieces * piece, core_send)
+    if inner > 1:
+        await_all(w_buf.at[pl.ds(0, inner - 1)], w_send, w_recv.at[0], True)
+        await_all(b_buf.at[pl.ds(0, inner - 1)], b_send, b_recv.at[0], True)
+    ret[a * peers + me] = part[a * peers + me]
+    await_all(ret.at[pl.ds(0, outer * peers - 1)], p_send, p_recv.at[0], False)
     for pp in range(peers):
-        total = ret[0, pp]
+        total = ret[pp]
         for aa in range(1, outer):
-            total += ret[aa, pp]
+            total += ret[aa * peers + pp]
         out_ref[pp * towers : (pp + 1) * towers] = total
-    for aa in range(outer):
-        for pp in range(peers):
-            mine = (a == aa) & (me == pp)
-            pl.when(jnp.logical_not(mine))(lambda aa=aa, pp=pp: send_part(aa, pp).wait_send())
+    await_all(part.at[pl.ds(0, outer * peers - 1)], p_send, p_recv.at[0], True)
 
 
 def shards(features, task_mask, tower_in, tower_bias, tower_head, head_bias):
@@ -445,24 +443,23 @@
         + [pl.BlockSpec(memory_space=pltpu.SMEM)],
         out_specs=pl.BlockSpec(memory_space=pltpu.VMEM),
         scratch_shapes=[
-            pltpu.VMEM((outer, ys, rows // LANES, 2, LANES, depth), features.dtype),
+            pltpu.VMEM((outer * peers * rows, depth), features.dtype),
             pltpu.VMEM((inner, towers, hidden, depth), tower_in.dtype),
             pltpu.VMEM((inner, 2, towers, hidden), tower_bias.dtype),
             pltpu.VMEM((inner, 2, towers, hidden, LANES), jnp.float32),
-            pltpu.VMEM((outer, peers, towers, rows), jnp.float32),
-            pltpu.VMEM((outer, peers, towers, rows), jnp.float32),
-            dma((rows // LANES,)),
-            dma((3,)),
-            dma((outer, peers, pieces)),
-            dma((2, outer, ys, pieces)),
-            dma((outer, max(1, ys - 1), pieces)),
-            dma((outer, ys, pieces)),
-            dma((max(1, inner - 1), towers)),
-            dma((inner, towers)),
-            dma((max(1, inner - 1),)),
-            dma((inner,)),
-            dma((outer, peers)),
-            dma((outer, peers)),
+            pltpu.VMEM((outer * peers, towers, rows), jnp.float32),
+            pltpu.VMEM((outer * peers, towers, rows), jnp.float32),
+            dma((rows // LANES + 3,)),
+            dma((2, plan(outer, pieces)[0])),
+            dma((outer * ys * rows // LANES,)),
+            dma((1,)),
+            dma((1,)),
+            dma((1,)),
+            dma((towers,)),
+            dma((1,)),
+            dma((1,)),
+            dma((1,)),
+            dma((1,)),
         ],
         compiler_params=pltpu.CompilerParams(
             collective_id=0, has_side_effects=True, vmem_limit_bytes=60 * 1024 * 1024

time: 79.8 us -> 74 us (0.927)
  Pallas kernels: 78.2 us -> 72.4 us
    pallas_call x1, Pallas kernels: 78.2 us -> 72.4 us  [shards(): pl.pallas_call(functools.partial(kernel, outer, inner, peers), out_shape=...]
where the time goes in v2:
time: 74 us; the launch traced here: 73.8 us
  Pallas kernels  72.4 us (98%)
  other arithmetic  1.35 us (2%)
    pallas_call x1, Pallas kernels, shards(): pl.pallas_call(functools.partial(kernel, outer, inner, peers), out_shape=...  72.4 us

profile of v2, /device:TPU:0, one launch (start us, length us, event | category | flops | bytes accessed | tf_op | source)
XLA Modules:
  0.0 73.8 jit_solution(17762852332602532713)
XLA Ops:
  0.0 0.0 copy-start
  0.0 72.4 %shard_map.64 = f32[16,384]{1,0:T(8,128)} custom-call(bf16[384,1024]{1,0:T(8,128)(2,1)} %feat_ref.1, bf16[4,256,1024]{2,1,0:T(8,128)(2,1)} %weight_ref.1, bf16[4,256]{1,0:T(4,128)(2,1)} %bias_ref.1, bf16[4,256]{1,0:T(4,128)(2,1)} %head_ref.1, f32[4]{0:T(128)} %hbias_ref.1), custom_call_target="tpu_custom_call" | custom-call | tf_op jit(solution)/shard_map/pallas_call | solution.py:439
  72.4 0.0 copy-done
  72.4 1.4 %bitcast_select_fusion = f32[384,16]{0,1:T(8,128)} fusion(f32[16,384]{1,0:T(8,128)} %shard_map.64, s32[384]{0:T(512)S(1)} %copy-done), kind=kLoop, calls=%fused_computation | loop fusion | flops 24576 | bytes 50688 | tf_op jit(solution)/shard_map/jit(_where)/select_n | solution.py:470
Async XLA Ops:
  0.0 72.4 %copy-start = (s32[384]{0:T(512)S(1)}, s32[384]{0:T(512)}, u32[]{:S(2)}) copy-start(s32[384]{0:T(512)} %param.7) | copy-start | bytes 4612

commit v3 on v2

--- a/solution.py
+++ b/solution.py
@@ -11,7 +11,7 @@
 LANES = 128
 PIECE_ROWS = 64
 LAG = 3
-SLOT_TASKS = 14
+SLOT_TASKS = 16
 
 
 def split_of_group(group, peers, weight_bytes, sample_bytes):
@@ -31,6 +31,10 @@
 
 
 def plan(outer, pieces):
+    def late(a, aa, h):
+        held = a in (0, outer - 1) and h == pieces - 2 and abs(aa - a) in (1, 2)
+        return held, -abs(aa - a) if held else 0
+
     avail = [{(a, 0, h): 0 for h in range(pieces)} for a in range(outer)]
     sends = [{} for _ in range(outer)]
     arrivals = [{} for _ in range(outer)]
@@ -39,12 +43,11 @@
     while any(len(have) < outer * pieces * 2 for have in avail):
         moves = []
         for a in range(outer):
-            ends = a in (0, outer - 1)
             for way, to in ((0, a + 1), (1, a - 1)):
                 if not 0 <= to < outer:
                     continue
                 ready = [
-                    (k, k and abs(aa - to) == 1, abs(aa - to), h, (aa, k, h))
+                    (k, -abs(aa - to), h, (aa, k, h))
                     for (aa, k, h), since in avail[a].items()
                     if since <= slot
                     and (a, way, aa, k, h) not in done
@@ -54,7 +57,7 @@
                 if ready:
                     moves.append((a, way, to, min(ready)[-1]))
             ready = [
-                (ends and abs(aa - a) == 1 and h == pieces - 2, since, abs(aa - a), h, (aa, 0, h))
+                (*late(a, aa, h), since, h, (aa, 0, h))
                 for (aa, k, h), since in avail[a].items()
                 if since <= slot
                 and k == 0
@@ -150,12 +153,6 @@
     load_w = pltpu.make_async_copy(weight_ref, w_buf.at[i], load_sem.at[quads])
     load_b = pltpu.make_async_copy(bias_ref, b_buf.at[i, 0], load_sem.at[quads + 1])
     load_h = pltpu.make_async_copy(head_ref, b_buf.at[i, 1], load_sem.at[quads + 2])
-    for load in loads:
-        load.start()
-    load_w.start()
-    load_b.start()
-    load_h.start()
-
     barrier = pltpu.get_barrier_semaphore()
 
     def greet(to):
@@ -168,6 +165,11 @@
     for k in range(1, inner):
         greet(dev(a, lax.rem(i + k, inner), me))
     greet(dev(a, i, partner))
+    for load in loads:
+        load.start()
+    load_w.start()
+    load_b.start()
+    load_h.start()
     neighbours = sel([(at > 0) + (at + 1 < outer) + ys + inner - 1 for at in range(outer)])
 
     def column(k):
@@ -268,7 +270,7 @@
             pl.when(jnp.logical_not(mine))(lambda pp=pp: send_part(aa, pp).start())
 
     slots, sends, arrivals, avail = plan(outer, pieces)
-    ready_far = [-(-hidden * max(inner - 1, 1) * (t + 1) // piece) + 2 for t in range(towers)]
+    ready_far = [-(-hidden * max(inner - 1, 1) * (t + 1) // piece) + 1 for t in range(towers)]
     orders, own, far = tasks_of(outer, ys, pieces, towers, ready_far, avail)
     steps = len(own)
     done_at = {}
@@ -384,16 +386,14 @@
     for s in range(1, steps):
         for u in own[s]:
             settle(u)
+        for u in own[s]:
             for t in range(towers):
                 compute(group_of(u), i, t, True)
-        if s > slots:
-            far_tasks(s)
         take(s - 2)
         start_sends(s + 1)
         if s == 2:
             biases_arrived()
-        if s <= slots:
-            far_tasks(s)
+        far_tasks(s)
         ended = []
         for at in range(outer):
             pairs = {}
@@ -438,7 +438,7 @@
     dma = pltpu.SemaphoreType.DMA
     logits = pl.pallas_call(
         functools.partial(kernel, outer, inner, peers),
-        out_shape=jax.ShapeDtypeStruct((peers * towers, rows), jnp.float32),
+        out_shape=pltpu.VMEM((peers * towers, rows), jnp.float32),
         in_specs=[pl.BlockSpec(memory_space=pl.ANY)] * 4
         + [pl.BlockSpec(memory_space=pltpu.SMEM)],
         out_specs=pl.BlockSpec(memory_space=pltpu.VMEM),

time: 74 us -> 71.5 us (0.966)
  Pallas kernels: 72.4 us -> 70.3 us
    pallas_call x1, Pallas kernels: 72.4 us -> 70.3 us  [shards(): pl.pallas_call(functools.partial(kernel, outer, inner, peers), out_shape=...]
where the time goes in v3:
time: 71.5 us; the launch traced here: 71 us
  Pallas kernels  70.3 us (98%)
    pallas_call x1, Pallas kernels, shards(): pl.pallas_call(functools.partial(kernel, outer, inner, peers), out_shape=...  70.3 us

profile of v3, /device:TPU:0, one launch (start us, length us, event | category | flops | bytes accessed | tf_op | source)
XLA Modules:
  0.0 71.0 jit_solution(1643352987704278479)
XLA Ops:
  0.0 0.0 copy-start
  0.0 70.3 %shard_map.64 = f32[16,384]{1,0:T(8,128)S(1)} custom-call(bf16[384,1024]{1,0:T(8,128)(2,1)} %feat_ref.1, bf16[4,256,1024]{2,1,0:T(8,128)(2,1)} %weight_ref.1, bf16[4,256]{1,0:T(4,128)(2,1)} %bias_ref.1, bf16[4,256]{1,0:T(4,128)(2,1)} %head_ref.1, f32[4]{0:T(128)} %hbias_ref.1), custom_call_target="tpu_custom_call" | custom-call | tf_op jit(solution)/shard_map/pallas_call | solution.py:439
  70.4 0.0 copy-done
  70.4 0.6 bitcast_select_fusion
Async XLA Ops:
  0.0 70.4 %copy-start = (s32[384]{0:T(512)S(1)}, s32[384]{0:T(512)}, u32[]{:S(2)}) copy-start(s32[384]{0:T(512)} %param.7) | copy-start | bytes 4612

commit v4 on v3

--- a/solution.py
+++ b/solution.py
@@ -71,7 +71,7 @@
             sends[a].setdefault((slot, way), (aa, k, h))
             got = (aa, 1 if way == 2 else k, h)
             avail[to][got] = slot + LAG
-            arrivals[to].setdefault(slot, []).append((*got, way))
+            arrivals[to].setdefault(slot, []).append(got)
         slot += 1
     return slot, sends, arrivals, avail
 
@@ -106,7 +106,7 @@
 def kernel(
     outer, inner, peers,
     feat_ref, weight_ref, bias_ref, head_ref, hbias_ref, out_ref,
-    x_buf, w_buf, b_buf, c_buf, part, ret,
+    x_buf, w_buf, b_buf, c_buf, h_buf, part, ret,
     load_sem, x_recv, core_recv, x_send, core_send, w_send, w_recv, b_send, b_recv, p_send, p_recv,
 ):
     rows, depth = feat_ref.shape
@@ -146,13 +146,14 @@
 
     loads = [
         pltpu.make_async_copy(
-            feat_ref.at[pl.ds(q * LANES, LANES)], x_rows(a, y, q, c), load_sem.at[q]
+            feat_ref.at[pl.ds(q * LANES, LANES)], x_rows(a, y, q, c), load_sem.at[0]
         )
         for q in range(quads)
     ]
-    load_w = pltpu.make_async_copy(weight_ref, w_buf.at[i], load_sem.at[quads])
-    load_b = pltpu.make_async_copy(bias_ref, b_buf.at[i, 0], load_sem.at[quads + 1])
-    load_h = pltpu.make_async_copy(head_ref, b_buf.at[i, 1], load_sem.at[quads + 2])
+    load_w = pltpu.make_async_copy(weight_ref, w_buf.at[i], load_sem.at[1])
+    load_b = pltpu.make_async_copy(bias_ref, b_buf.at[i, 0], load_sem.at[2])
+    load_h = pltpu.make_async_copy(head_ref, b_buf.at[i, 1], load_sem.at[2])
+    load_s = pltpu.make_async_copy(hbias_ref, h_buf, load_sem.at[3])
     barrier = pltpu.get_barrier_semaphore()
 
     def greet(to):
@@ -170,6 +171,7 @@
     load_w.start()
     load_b.start()
     load_h.start()
+    load_s.start()
     neighbours = sel([(at > 0) + (at + 1 < outer) + ys + inner - 1 for at in range(outer)])
 
     def column(k):
@@ -184,11 +186,11 @@
 
     def along(way, aa, k, h, slot):
         to = lax.rem(a + 1, outer) if way == 0 else lax.rem(a + outer - 1, outer)
-        return send_x(aa, column(k), h, x_send.at[0], x_recv.at[0, slot], dev(to, i, me))
+        return send_x(aa, column(k), h, x_send.at[0], x_recv.at[slot], dev(to, i, me))
 
     def across(aa, k, h, slot):
         to = dev(a, i, lax.rem(y + k, ys) * 2 + c)
-        return send_x(aa, y, h, x_send.at[0], x_recv.at[1, slot], to)
+        return send_x(aa, y, h, x_send.at[0], x_recv.at[slot], to)
 
     def sibling(aa, k, h):
         sem = core_recv.at[at_group(aa, column(k), h // per)]
@@ -251,7 +253,7 @@
             v = jnp.maximum(pre[:, cc * LANES : (cc + 1) * LANES] + bias, 0.0) * head
             total = jnp.sum(v, axis=0, keepdims=True)
             if first:
-                total += jnp.where(a == 0, hbias_ref[t], 0.0)
+                total += jnp.where(a == 0, h_buf[t], 0.0)
             else:
                 total += part[aa * peers + yy * 2 + cc, pl.ds(t, 1), lanes]
             part[aa * peers + yy * 2 + cc, pl.ds(t, 1), lanes] = total
@@ -316,25 +318,23 @@
 
     def take(slot):
         lists = [arrivals[at].get(slot, []) for at in range(outer)]
-        for link in range(2):
-            kept = [[e for *e, way in x if (way == 2) == (link == 1)] for x in lists]
-            counts = [sum(ys - 1 if k else 1 for _, k, _ in x) for x in kept]
-            by_count(counts, lambda n: await_rows(n * piece, x_recv.at[link, slot]))
-            for n in range(max(len(x) for x in kept)):
-                for kind in range(2):
-                    flags = [len(x) > n and x[n][1] == kind for x in kept]
-                    if not any(flags):
-                        continue
-                    some = next(x[n] for x, f in zip(kept, flags) if f)
-                    entries = [x[n] if f else some for x, f in zip(kept, flags)]
-                    aa = sel([e[0] for e in entries])
-                    h = sel([e[2] for e in entries])
-
-                    def relay(aa=aa, h=h, kind=kind):
-                        for k in range(1, ys) if kind else (0,):
-                            sibling(aa, k, h).start()
-
-                    when(flags, relay)
+        counts = [sum(ys - 1 if k else 1 for _, k, _ in x) for x in lists]
+        by_count(counts, lambda n: await_rows(n * piece, x_recv.at[slot]))
+        for n in range(max(len(x) for x in lists)):
+            for kind in range(2):
+                flags = [len(x) > n and x[n][1] == kind for x in lists]
+                if not any(flags):
+                    continue
+                some = next(x[n] for x, f in zip(lists, flags) if f)
+                entries = [x[n] if f else some for x, f in zip(lists, flags)]
+                aa = sel([e[0] for e in entries])
+                h = sel([e[2] for e in entries])
+
+                def relay(aa=aa, h=h, kind=kind):
+                    for k in range(1, ys) if kind else (0,):
+                        sibling(aa, k, h).start()
+
+                when(flags, relay)
 
     def settle(u):
         await_rows(LANES, core_recv.at[at_group(*group_of(u))])
@@ -350,12 +350,11 @@
             columns(lax.rem(i + k, inner))
 
     pl.semaphore_wait(barrier, neighbours)
-    for load in loads:
-        load.wait()
+    pltpu.make_async_copy(feat_ref, x_buf.at[pl.ds(0, rows)], load_sem.at[0]).wait()
     start_sends(0)
     start_sends(1)
-    load_b.wait()
-    load_h.wait()
+    pltpu.make_async_copy(b_buf.at[i], b_buf.at[i], load_sem.at[2]).wait()
+    load_s.wait()
     for k in range(1, inner):
         send_b(k).start()
     load_w.wait()
@@ -439,18 +438,18 @@
     logits = pl.pallas_call(
         functools.partial(kernel, outer, inner, peers),
         out_shape=pltpu.VMEM((peers * towers, rows), jnp.float32),
-        in_specs=[pl.BlockSpec(memory_space=pl.ANY)] * 4
-        + [pl.BlockSpec(memory_space=pltpu.SMEM)],
+        in_specs=[pl.BlockSpec(memory_space=pl.ANY)] * 5,
         out_specs=pl.BlockSpec(memory_space=pltpu.VMEM),
         scratch_shapes=[
             pltpu.VMEM((outer * peers * rows, depth), features.dtype),
             pltpu.VMEM((inner, towers, hidden, depth), tower_in.dtype),
             pltpu.VMEM((inner, 2, towers, hidden), tower_bias.dtype),
             pltpu.VMEM((inner, 2, towers, hidden, LANES), jnp.float32),
+            pltpu.SMEM((towers,), jnp.float32),
             pltpu.VMEM((outer * peers, towers, rows), jnp.float32),
             pltpu.VMEM((outer * peers, towers, rows), jnp.float32),
-            dma((rows // LANES + 3,)),
-            dma((2, plan(outer, pieces)[0])),
+            dma((4,)),
+            dma((plan(outer, pieces)[0],)),
             dma((outer * ys * rows // LANES,)),
             dma((1,)),
             dma((1,)),

time: 71.5 us -> 70.5 us (0.986)
  Pallas kernels: 70.3 us -> 69.3 us
    pallas_call x1, Pallas kernels: 70.3 us -> 69.3 us  [shards(): pl.pallas_call(functools.partial(kernel, outer, inner, peers), out_shape=...]
where the time goes in v4:
time: 70.5 us; the launch traced here: 70 us
  Pallas kernels  69.3 us (98%)
    pallas_call x1, Pallas kernels, shards(): pl.pallas_call(functools.partial(kernel, outer, inner, peers), out_shape=...  69.3 us

profile of v4, /device:TPU:0, one launch (start us, length us, event | category | flops | bytes accessed | tf_op | source)
XLA Modules:
  0.0 70.0 jit_solution(16524360516180197406)
XLA Ops:
  0.0 0.0 copy-start
  0.0 69.3 %shard_map.64 = f32[16,384]{1,0:T(8,128)S(1)} custom-call(bf16[384,1024]{1,0:T(8,128)(2,1)} %feat_ref.1, bf16[4,256,1024]{2,1,0:T(8,128)(2,1)} %weight_ref.1, bf16[4,256]{1,0:T(4,128)(2,1)} %bias_ref.1, bf16[4,256]{1,0:T(4,128)(2,1)} %head_ref.1, f32[4]{0:T(128)} %hbias_ref.1), custom_call_target="tpu_custom_call" | custom-call | tf_op jit(solution)/shard_map/pallas_call | solution.py:438
  69.3 0.0 copy-done
  69.3 0.6 bitcast_select_fusion
Async XLA Ops:
  0.0 69.3 %copy-start = (s32[384]{0:T(512)S(1)}, s32[384]{0:T(512)}, u32[]{:S(2)}) copy-start(s32[384]{0:T(512)} %param.7) | copy-start | bytes 4612

commit v5 on v4

--- a/solution.py
+++ b/solution.py
@@ -192,9 +192,8 @@
         to = dev(a, i, lax.rem(y + k, ys) * 2 + c)
         return send_x(aa, y, h, x_send.at[0], x_recv.at[slot], to)
 
-    def sibling(aa, k, h):
-        sem = core_recv.at[at_group(aa, column(k), h // per)]
-        return send_x(aa, column(k), h, core_send.at[0], sem, dev(a, i, partner))
+    def sibling(aa, k, h, used):
+        return send_x(aa, column(k), h, core_send.at[0], core_recv.at[used], dev(a, i, partner))
 
     def await_rows(count, sem):
         ref = x_buf.at[pl.ds(0, count)]
@@ -281,6 +280,14 @@
             done_at[u] = s
         for u, _ in far[s]:
             done_at[u] = s
+
+    used_steps = [s for s in range(steps) if own[s]]
+    used_at = [
+        {order[u]: n for n, s in enumerate(used_steps) for u in own[s]} for order in orders
+    ]
+
+    def used_by(entries, k):
+        return sel([used_at[at][e[0], k, e[2] // per] for at, e in enumerate(entries)])
 
     def group_of(u):
         aa = sel([orders[at][u][0] for at in range(outer)])
@@ -330,14 +337,14 @@
                 aa = sel([e[0] for e in entries])
                 h = sel([e[2] for e in entries])
 
-                def relay(aa=aa, h=h, kind=kind):
+                def relay(aa=aa, h=h, kind=kind, entries=entries):
                     for k in range(1, ys) if kind else (0,):
-                        sibling(aa, k, h).start()
+                        sibling(aa, k, h, used_by(entries, k)).start()
 
                 when(flags, relay)
 
-    def settle(u):
-        await_rows(LANES, core_recv.at[at_group(*group_of(u))])
+    def settle(s):
+        await_rows(len(own[s]) * LANES, core_recv.at[used_steps.index(s)])
 
     def weights_arrived(t):
         if inner > 1:
@@ -363,7 +370,7 @@
             send_w(k, t).start()
     columns(i)
     for h in range(pieces):
-        sibling(a, 0, h).start()
+        sibling(a, 0, h, used_by([(at, 0, h) for at in range(outer)], 0)).start()
 
     weights = set()
     def far_tasks(s):
@@ -383,8 +390,8 @@
                 lax.fori_loop(1, inner, each, 0)
 
     for s in range(1, steps):
-        for u in own[s]:
-            settle(u)
+        if own[s]:
+            settle(s)
         for u in own[s]:
             for t in range(towers):
                 compute(group_of(u), i, t, True)
@@ -434,6 +441,9 @@
     outer = group // inner
     ys = peers // 2
     pieces = rows // PIECE_ROWS
+    slots, _, _, avail = plan(outer, pieces)
+    own = tasks_of(outer, ys, pieces, towers, [0] * towers, avail)[1]
+    used = sum(1 for groups in own if groups)
     dma = pltpu.SemaphoreType.DMA
     logits = pl.pallas_call(
         functools.partial(kernel, outer, inner, peers),
@@ -449,8 +459,8 @@
             pltpu.VMEM((outer * peers, towers, rows), jnp.float32),
             pltpu.VMEM((outer * peers, towers, rows), jnp.float32),
             dma((4,)),
-            dma((plan(outer, pieces)[0],)),
-            dma((outer * ys * rows // LANES,)),
+            dma((slots,)),
+            dma((used,)),
             dma((1,)),
             dma((1,)),
             dma((1,)),

time: 70.5 us -> 70.4 us (level)
  no operation moved by 1% of the time
where the time goes in v5:
time: 70.4 us; the launch traced here: 69.8 us
  Pallas kernels  69.2 us (98%)
    pallas_call x1, Pallas kernels, shards(): pl.pallas_call(functools.partial(kernel, outer, inner, peers), out_shape=...  69.2 us

profile of v5, /device:TPU:0, one launch (start us, length us, event | category | flops | bytes accessed | tf_op | source)
XLA Modules:
  0.0 69.8 jit_solution(15555495953468005482)
XLA Ops:
  0.0 0.0 copy-start
  0.0 69.2 %shard_map.64 = f32[16,384]{1,0:T(8,128)S(1)} custom-call(bf16[384,1024]{1,0:T(8,128)(2,1)} %feat_ref.1, bf16[4,256,1024]{2,1,0:T(8,128)(2,1)} %weight_ref.1, bf16[4,256]{1,0:T(4,128)(2,1)} %bias_ref.1, bf16[4,256]{1,0:T(4,128)(2,1)} %head_ref.1, f32[4]{0:T(128)} %hbias_ref.1), custom_call_target="tpu_custom_call" | custom-call | tf_op jit(solution)/shard_map/pallas_call | solution.py:448
  69.2 0.0 copy-done
  69.2 0.6 bitcast_select_fusion
Async XLA Ops:
  0.0 69.2 %copy-start = (s32[384]{0:T(512)S(1)}, s32[384]{0:T(512)}, u32[]{:S(2)}) copy-start(s32[384]{0:T(512)} %param.7) | copy-start | bytes 4612
